TPU v7x, 32 devices: a whole 2x2x4 slice. The times are simulated.
32 devices in a mesh: dp: 4 (over y, x), vocab: 8 (over z, core).
Axes of the slice: x: 2, y: 2, z: 4, core: 2. Of those that a mesh axis runs over, the one named last changes fastest.
Arguments:
- token_ids: int32 [131072], P(('dp', 'vocab')), may hold values from 0 to 7679, as said below
- valid_counts: int32 [1024], P(('dp', 'vocab')), may hold values from 64 to 128
- grad_output: bfloat16 [131072, 768], P(('dp', 'vocab')), may hold values from -6 to 6
- pre_norm: bfloat16 [131072, 768], P(('dp', 'vocab')), may hold values from -6 to 6
- norm_gain: float32 [768], replicated, may hold values from 0.5 to 1.5
Outputs:
- grad_table: float32 [7680, 768], P('vocab')
Inputs may be any that keep to these rules, and one draw needn't show every extreme that they name: `token_ids`: of the 4096 positions of one device, at most 1024 have ids in any one range [k * 960, (k + 1) * 960); in every group of 8 consecutive devices one such range takes exactly 1024 from every device of the group. Padding positions carry ids too.
All inputs are finite; a program needn't handle non-finite values.
Results may differ from a plain program's by a relative error of at most 0.0029.
Values may be sent and summed in bfloat16 or wider, within the bound.
No kernel may reach another device: no remote copies, remote signals or barrier semaphores. Data moves between devices by JAX's collectives and lax.ppermute only.
A program may use at most 128 MiB of HBM per device.

v0:
```python
import jax
import jax.numpy as jnp
from jax import lax
from jax.sharding import PartitionSpec as P

VOCAB_DEV = 960
BLOCK = 128


def row_grads(grads, values, counts, gain):
    x = values.astype(jnp.float32)
    mu = jnp.mean(x, axis=1, keepdims=True)
    centered_input = x - mu
    inverse_deviation = lax.rsqrt(
        jnp.mean(centered_input * centered_input, axis=1, keepdims=True) + 1e-12
    )
    normalized_input = centered_input * inverse_deviation
    scaled_gradient = gain[None, :] * grads.astype(jnp.float32)
    first_term = jnp.mean(scaled_gradient, axis=1, keepdims=True)
    second_term = jnp.mean(scaled_gradient * normalized_input, axis=1, keepdims=True)
    input_gradient = inverse_deviation * (
        scaled_gradient - first_term - normalized_input * second_term
    )
    place = jnp.arange(x.shape[0], dtype=jnp.int32) % BLOCK
    alive = place < jnp.repeat(counts, BLOCK)
    return (jnp.where(alive[:, None], input_gradient, 0.0).astype(jnp.bfloat16), alive)


def per_device(token_ids, valid_counts, grad_output, pre_norm, norm_gain):
    tok_count = token_ids.shape[0]
    width = grad_output.shape[1]
    shards = lax.axis_size("vocab")
    per_owner = 2 * tok_count // shards
    rows, alive = row_grads(grad_output, pre_norm, valid_counts, norm_gain)
    owner = token_ids // VOCAB_DEV
    within = token_ids % VOCAB_DEV
    marks = (owner[:, None] == jnp.arange(shards, dtype=jnp.int32)[None, :]).astype(jnp.int32)
    rank = jnp.sum((jnp.cumsum(marks, axis=0) - 1) * marks, axis=1)
    target = owner * per_owner + rank
    outbox = jnp.zeros((shards * per_owner, width), jnp.bfloat16).at[target].set(rows)
    labels = (
        jnp.full((shards * per_owner,), -1, jnp.int32).at[target].set(jnp.where(alive, within, -1))
    )
    outbox = outbox.reshape(shards, per_owner, width)
    labels = labels.reshape(shards, per_owner)
    inlabels = lax.all_to_all(labels, "vocab", split_axis=0, concat_axis=0, tiled=True).reshape(
        shards * per_owner
    )
    picker = (jnp.arange(VOCAB_DEV, dtype=jnp.int32)[:, None] == inlabels[None, :]).astype(
        jnp.bfloat16
    )
    piece = lax.all_to_all(outbox, "vocab", split_axis=0, concat_axis=0, tiled=True)
    flat = piece.reshape(piece.shape[0] * piece.shape[1], piece.shape[2])
    partial_table = jnp.dot(picker, flat, preferred_element_type=jnp.float32)
    table = lax.psum(partial_table, "dp")
    return table


def solution(mesh):
    in_specs = (
        P(("dp", "vocab")),
        P(("dp", "vocab")),
        P(("dp", "vocab"), None),
        P(("dp", "vocab"), None),
        P(),
    )
    out_specs = P("vocab", None)
    return jax.shard_map(
        per_device, mesh=mesh, in_specs=in_specs, out_specs=out_specs, check_vma=False
    )
```

profile of v0, /device:TPU:0, one launch (start us, length us, event | category | flops | bytes accessed | tf_op | source)
XLA Modules:
  0.0 463.4 jit_solution(11556045148350424511)
XLA Ops:
  6.5 0.7 add_select_fusion.2
  7.3 2.3 reduce-window.6
  9.6 0.3 slice_reduce_fusion
  9.9 0.2 reduce-window.9
  10.1 0.1 add_bitcast_fusion
  10.2 0.1 fusion.24
  10.3 0.8 fusion.27
  11.1 16.1 %scatter_custom_fusion = s32[8192]{0:T(1024)} fusion(s32[4096]{0:T(1024)S(1)} %get-tuple-element.8, s32[4096]{0:T(1024)S(1)} %get-tuple-element.7, s32[]{:T(128)} %constant.49.clone.1), kind=kCustom, calls=%fused_computation.47 | custom fusion | bytes 32772 | tf_op jit(solution)/shard_map/scatter | solution.py:42
  27.2 6.4 %all-to-all-start = ((s32[8,1,1024]{2,1,0:T(1,128)}), s32[8,1,1024]{2,1,0:T(1,128)S(1)}, u32[]{:S(2)}, u32[]{:S(2)}) async-start(s32[8,1,1024]{2,1,0:T(1,128)} %bitcast.3), calls=%async_computation | async-start | bytes 65536 | tf_op jit(solution)/shard_map/all_to_all | solution.py:46
  33.6 0.0 all-reduce.2.cloned.1.call-start
  33.6 0.0 copy-start
  33.7 0.0 copy-start.1
  33.7 3.8 convert_reduce_fusion
  37.5 5.4 %fusion.11 = f32[4096]{0:T(1024)S(1)} fusion(bf16[4096,768]{1,0:T(8,128)(2,1)} %param.8, f32[4096]{0:T(1024)S(1)} %broadcast_multiply_fusion.2), kind=kLoop, calls=%fused_computation.16 | loop fusion | flops 12578816 | bytes 6324224 | tf_op jit(solution)/shard_map/reduce_sum | solution.py:15
  43.0 0.0 copy-done.2
  43.0 4.7 %fusion.12 = (f32[4096]{0:T(1024)S(1)}, f32[4096]{0:T(1024)S(1)}) fusion(bf16[4096,768]{1,0:T(8,128)(2,1)S(1)} %copy-done.1, f32[768]{0:T(1024)S(1)} %copy-done.2, f32[4096]{0:T(1024)S(1)} %add_rsqrt_fusion, f32[4096]{0:T(1024)S(1)} %broadcast_multiply_fusion.2, bf16[4096,768]{1,0:T(8,128)(2,1)S(1)} %copy-done), kind=kLoop, calls=%fused_computation.18 | loop fusion | flops 25157632 | bytes 12651520 | tf_op jit(solution)/shard_map/reduce_sum | solution.py:19
  47.7 0.1 fusion.26
  47.8 28.5 %scatter_custom_fusion.1 = bf16[8192,768]{1,0:T(8,128)(2,1)} fusion(s32[4096]{0:T(1024)S(1)} %get-tuple-element.8, bf16[4096,768]{1,0:T(8,128)(2,1)} %param.8, bf16[4096,768]{1,0:T(8,128)(2,1)} %param.7, f32[]{:T(128)} %constant.58.clone.1, f32[4096]{0:T(1024)S(1)} %get-tuple-element.11, f32[4096]{0:T(1024)S(1)} %get-tuple-element.12, ...), kind=kCustom, calls=%fused_computation.19 | custom fusion | flops 31457280 | bytes 25239558 | tf_op jit(solution)/shard_map/scatter | solution.py:40
  76.2 0.0 all-to-all-done
  76.2 278.8 %all_to_all.14 = bf16[8,1024,768]{2,1,0:T(8,128)(2,1)S(1)} all-to-all(bf16[8,1024,768]{2,1,0:T(8,128)(2,1)} %bitcast.28), channel_id=1, replica_groups=mesh['dp'=4,'vocab'=8] {'vocab'}, dimensions={0} | all-to-all | bytes 25165824 | tf_op jit(solution)/shard_map/all_to_all | solution.py:52
  355.0 15.1 %fusion = f32[960,768]{1,0:T(8,128)} fusion(bf16[8192,768]{1,0:T(8,128)(2,1)S(1)} %bitcast.29, s32[8192]{0:T(1024)S(1)} %bitcast.30), kind=kOutput, calls=%fused_computation.3 | convolution fusion | flops 12087459840 | bytes 15564800 | tf_op jit(solution)/shard_map/dot_general | solution.py:54
  370.1 0.0 all-reduce.2.cloned.1.call-update
  370.1 82.8 %all-reduce.2.cloned.1.call-done = f32[960,768]{1,0:T(8,128)} async-done(((f32[960,768]{1,0:T(8,128)}), f32[960,768]{1,0:T(8,128)}) %all-reduce.2.cloned.1.call-update) | async-done | bytes 2949136 | tf_op jit(solution)/shard_map/psum | solution.py:55
  452.9 3.6 copy.9
  (9 shorter events, 0.0 us)
Async XLA Ops:
  6.5 36.4 %copy-start.2 = (f32[768]{0:T(1024)S(1)}, f32[768]{0:T(1024)}, u32[]{:S(2)}) copy-start(f32[768]{0:T(1024)} %param.9) | copy-start | bytes 9220
  27.2 49.0 %all-to-all-start = ((s32[8,1,1024]{2,1,0:T(1,128)}), s32[8,1,1024]{2,1,0:T(1,128)S(1)}, u32[]{:S(2)}, u32[]{:S(2)}) async-start(s32[8,1,1024]{2,1,0:T(1,128)} %bitcast.3), calls=%async_computation | async-start | bytes 65536 | tf_op jit(solution)/shard_map/all_to_all | solution.py:46
  33.6 14.1 %copy-start.3 = (s32[32]{0:T(128)S(1)}, s32[32]{0:T(128)}, u32[]{:S(2)}) copy-start(s32[32]{0:T(128)} %param.6) | copy-start | bytes 388
  33.6 419.3 %all-reduce.2.cloned.1.call-start = ((), (), s32[]{:S(2)}) async-start(), calls=%async_computation.2 | async-start | bytes 5898240 | tf_op jit(solution)/shard_map/psum | solution.py:55
  33.6 9.3 %copy-start = (bf16[4096,768]{1,0:T(8,128)(2,1)S(1)}, bf16[4096,768]{1,0:T(8,128)(2,1)}, u32[]{:S(2)}) copy-start(bf16[4096,768]{1,0:T(8,128)(2,1)} %param.8) | copy-start | bytes 18874372
  33.7 9.3 %copy-start.1 = (bf16[4096,768]{1,0:T(8,128)(2,1)S(1)}, bf16[4096,768]{1,0:T(8,128)(2,1)}, u32[]{:S(2)}) copy-start(bf16[4096,768]{1,0:T(8,128)(2,1)} %param.7) | copy-start | bytes 18874372
Sparse Core Ops, SparseCore 0:
  370.3 82.5 all-reduce.1
where the time goes:
time: 464 us; the launch traced here: 463 us
  blocking collectives  279 us (60%)
  waiting for transfers between devices  82.8 us (18%)
  other arithmetic  46.7 us (10%)
  local copies, waits for them, and re-layouts  20 us (4%)
  matrix products  15.1 us (3%)
  between operations  13.5 us (3%)
  starting transfers between devices  6.39 us (1%)
    all_to_all x1, blocking collectives, per_device(): lax.all_to_all(outbox, 'vocab', split_axis=0, concat_axis=0, tiled=True)  279 us
    psum x1, waiting for transfers between devices, per_device(): table = lax.psum(partial_table, 'dp')  82.8 us
    scatter x1, other arithmetic, per_device(): jnp.zeros((shards * per_owner, width), jnp.bfloat16).at[target].set(rows)  28.5 us
    scatter x1, local copies, waits for them, and re-layouts, per_device(): jnp.full((shards * per_owner,), -1, jnp.int32).at[target]  16.1 us
    dot_general x1, matrix products, per_device(): partial_table = jnp.dot(picker, flat, preferred_element_type=jnp.float32)  15.1 us
  transfers between devices with their start and end apart: 2, of which 1 were waited for; matrix products, arithmetic and copies ran while one was open for 9% of the time, Pallas kernels for 0%

commit v1 on v0

--- a/solution.py
+++ b/solution.py
@@ -52,7 +52,9 @@
     piece = lax.all_to_all(outbox, "vocab", split_axis=0, concat_axis=0, tiled=True)
     flat = piece.reshape(piece.shape[0] * piece.shape[1], piece.shape[2])
     partial_table = jnp.dot(picker, flat, preferred_element_type=jnp.float32)
-    table = lax.psum(partial_table, "dp")
+    table = partial_table
+    for hop in (1, 2):
+        table = table + lax.ppermute(table, "dp", [(dev, dev ^ hop) for dev in range(4)])
     return table
 
 

time: 464 us -> 495 us (1.067)
  waiting for transfers between devices: 82.8 us -> 127 us
  between operations: 13.5 us -> 0.15 us
    ppermute x0 -> x2, waiting for transfers between devices: none -> 127 us  [per_device(): lax.ppermute(table, 'dp', [(dev, dev ^ hop) for dev in range(4)])]
    psum x1 -> x0, waiting for transfers between devices: 82.8 us -> none  [per_device(): table = lax.psum(partial_table, 'dp')]
  transfers between devices with their start and end apart: 2 -> 3, of which waited for: 1 -> 2; matrix products, arithmetic and copies ran while one was open for 9% -> 9% of each run, Pallas kernels for 0% -> 0%
where the time goes in v1:
time: 495 us; the launch traced here: 494 us
  blocking collectives  279 us (56%)
  waiting for transfers between devices  127 us (26%)
  other arithmetic  49.3 us (10%)
  local copies, waits for them, and re-layouts  16.4 us (3%)
  matrix products  13.5 us (3%)
  starting transfers between devices  9.5 us (2%)
    all_to_all x1, blocking collectives, per_device(): lax.all_to_all(outbox, 'vocab', split_axis=0, concat_axis=0, tiled=True)  279 us
    ppermute x2, waiting for transfers between devices, per_device(): lax.ppermute(table, 'dp', [(dev, dev ^ hop) for dev in range(4)])  127 us
    scatter x1, other arithmetic, per_device(): jnp.zeros((shards * per_owner, width), jnp.bfloat16).at[target].set(rows)  28.5 us
    scatter x1, local copies, waits for them, and re-layouts, per_device(): jnp.full((shards * per_owner,), -1, jnp.int32).at[target]  16.1 us
    dot_general x1, matrix products, per_device(): partial_table = jnp.dot(picker, flat, preferred_element_type=jnp.float32)  13.5 us
  transfers between devices with their start and end apart: 3, of which 2 were waited for; matrix products, arithmetic and copies ran while one was open for 9% of the time, Pallas kernels for 0%

profile of v1, /device:TPU:0, one launch (start us, length us, event | category | flops | bytes accessed | tf_op | source)
XLA Modules:
  0.0 494.3 jit_solution(9127191938103784522)
XLA Ops:
  0.0 0.9 add_select_fusion.2
  0.9 2.3 reduce-window.6
  3.2 0.3 slice_reduce_fusion
  3.5 0.2 reduce-window.9
  3.7 0.1 add_bitcast_fusion
  3.8 0.1 fusion.24
  4.0 0.8 fusion.27
  4.7 16.1 %scatter_custom_fusion = s32[8192]{0:T(1024)} fusion(s32[4096]{0:T(1024)S(1)} %get-tuple-element.8, s32[4096]{0:T(1024)S(1)} %get-tuple-element.7, s32[]{:T(128)} %constant.49.clone.1), kind=kCustom, calls=%fused_computation.47 | custom fusion | bytes 32772 | tf_op jit(solution)/shard_map/scatter | solution.py:42
  20.8 6.4 %all-to-all-start = ((s32[8,1,1024]{2,1,0:T(1,128)}), s32[8,1,1024]{2,1,0:T(1,128)S(1)}, u32[]{:S(2)}, u32[]{:S(2)}) async-start(s32[8,1,1024]{2,1,0:T(1,128)} %bitcast.3), calls=%async_computation | async-start | bytes 65536 | tf_op jit(solution)/shard_map/all_to_all | solution.py:46
  27.2 0.0 copy-start
  27.2 0.0 copy-start.2
  27.2 3.8 convert_reduce_fusion
  31.1 5.5 %fusion.11 = f32[4096]{0:T(1024)S(1)} fusion(bf16[4096,768]{1,0:T(8,128)(2,1)} %param.8, f32[4096]{0:T(1024)S(1)} %broadcast_multiply_fusion.2), kind=kLoop, calls=%fused_computation.16 | loop fusion | flops 12578816 | bytes 6324224 | tf_op jit(solution)/shard_map/reduce_sum | solution.py:15
  36.6 4.7 fusion.12
  41.3 0.1 fusion.26
  41.4 28.5 %scatter_custom_fusion.1 = bf16[8192,768]{1,0:T(8,128)(2,1)} fusion(s32[4096]{0:T(1024)S(1)} %get-tuple-element.8, bf16[4096,768]{1,0:T(8,128)(2,1)} %param.8, bf16[4096,768]{1,0:T(8,128)(2,1)} %param.7, f32[]{:T(128)} %constant.58.clone.1, f32[4096]{0:T(1024)S(1)} %get-tuple-element.11, f32[4096]{0:T(1024)S(1)} %get-tuple-element.12, ...), kind=kCustom, calls=%fused_computation.19 | custom fusion | flops 31457280 | bytes 25239558 | tf_op jit(solution)/shard_map/scatter | solution.py:40
  69.8 278.8 %all_to_all.14 = bf16[8,1024,768]{2,1,0:T(8,128)(2,1)S(1)} all-to-all(bf16[8,1024,768]{2,1,0:T(8,128)(2,1)} %bitcast.30), channel_id=1, replica_groups=mesh['dp'=4,'vocab'=8] {'vocab'}, dimensions={0} | all-to-all | bytes 25165824 | tf_op jit(solution)/shard_map/all_to_all | solution.py:52
  348.7 13.5 %fusion = f32[960,768]{1,0:T(8,128)S(1)} fusion(bf16[8192,768]{1,0:T(8,128)(2,1)S(1)} %bitcast.31, s32[8192]{0:T(1024)S(1)} %bitcast.32), kind=kOutput, calls=%fused_computation.3 | convolution fusion | flops 12087459840 | bytes 15564800 | tf_op jit(solution)/shard_map/dot_general | solution.py:54
  362.2 1.6 collective-permute-start
  363.7 63.8 %collective-permute-done = f32[960,768]{1,0:T(8,128)S(1)} collective-permute-done((f32[960,768]{1,0:T(8,128)S(1)}, f32[960,768]{1,0:T(8,128)S(1)}, u32[]{:S(2)}, u32[]{:S(2)}) %collective-permute-start) | collective-permute-done | bytes 2949152 | tf_op jit(solution)/shard_map/ppermute | solution.py:57
  427.5 0.4 add.48
  427.9 1.6 collective-permute-start.1
  429.5 62.9 %collective-permute-done.1 = f32[960,768]{1,0:T(8,128)S(1)} collective-permute-done((f32[960,768]{1,0:T(8,128)S(1)}, f32[960,768]{1,0:T(8,128)S(1)}, u32[]{:S(2)}, u32[]{:S(2)}) %collective-permute-start.1) | collective-permute-done | bytes 2949152 | tf_op jit(solution)/shard_map/ppermute | solution.py:57
  492.4 2.0 add.49
  (14 shorter events, 0.0 us)
Async XLA Ops:
  0.0 36.6 %slice-start = ((s8[6291456]{0:T(1024)(128)(4,1)}), s8[2097152]{0:T(1024)(128)(4,1)S(1)}, s32[]{:S(2)}) async-start(s8[6291456]{0:T(1024)(128)(4,1)} %bitcast.28), calls=%async_computation.2 | async-start | bytes 4194304
  0.0 36.6 %copy-start.1 = (f32[768]{0:T(1024)S(1)}, f32[768]{0:T(1024)}, u32[]{:S(2)}) copy-start(f32[768]{0:T(1024)} %param.9) | copy-start | bytes 9220
  20.8 49.0 %all-to-all-start = ((s32[8,1,1024]{2,1,0:T(1,128)}), s32[8,1,1024]{2,1,0:T(1,128)S(1)}, u32[]{:S(2)}, u32[]{:S(2)}) async-start(s32[8,1,1024]{2,1,0:T(1,128)} %bitcast.3), calls=%async_computation | async-start | bytes 65536 | tf_op jit(solution)/shard_map/all_to_all | solution.py:46
  27.2 9.4 %slice-start.1 = ((s8[6291456]{0:T(1024)(128)(4,1)}), s8[4194304]{0:T(1024)(128)(4,1)S(1)}, s32[]{:S(2)}) async-start(s8[6291456]{0:T(1024)(128)(4,1)} %bitcast.28), calls=%async_computation.3 | async-start | bytes 8388608
  27.2 9.4 %copy-start = (bf16[4096,768]{1,0:T(8,128)(2,1)S(1)}, bf16[4096,768]{1,0:T(8,128)(2,1)}, u32[]{:S(2)}) copy-start(bf16[4096,768]{1,0:T(8,128)(2,1)} %param.7) | copy-start | bytes 18874372
  27.2 14.1 %copy-start.2 = (s32[32]{0:T(128)S(1)}, s32[32]{0:T(128)}, u32[]{:S(2)}) copy-start(s32[32]{0:T(128)} %param.6) | copy-start | bytes 388
  362.2 65.3 %collective-permute-start = (f32[960,768]{1,0:T(8,128)S(1)}, f32[960,768]{1,0:T(8,128)S(1)}, u32[]{:S(2)}, u32[]{:S(2)}) collective-permute-start(f32[960,768]{1,0:T(8,128)S(1)} %fusion), channel_id=1, source_target_pairs={{0,8},{8,0},{16,24},{24,16},{1,9},{9,1},{17,25},{25,17},{2,10},{10... | collective-permute-start | bytes 8847368 | tf_op jit(solution)/shard_map/ppermute | solution.py:57
  427.9 64.5 %collective-permute-start.1 = (f32[960,768]{1,0:T(8,128)S(1)}, f32[960,768]{1,0:T(8,128)S(1)}, u32[]{:S(2)}, u32[]{:S(2)}) collective-permute-start(f32[960,768]{1,0:T(8,128)S(1)} %add.48), channel_id=1, source_target_pairs={{0,16},{8,24},{16,0},{24,8},{1,17},{9,25},{17,1},{25,9},{2,18},{10... | collective-permute-start | bytes 8847368 | tf_op jit(solution)/shard_map/ppermute | solution.py:57
